TPU v7x, 32 devices: a whole 2x2x4 slice. The times are simulated.
32 devices in a mesh: own: 8 (over z, x), rep: 4 (over y, core).
Axes of the slice: x: 2, y: 2, z: 4, core: 2. Of those that a mesh axis runs over, the one named last changes fastest.
Arguments:
- block_pool: bfloat16 [2048, 64, 576], P(('own', 'rep')), may hold values from -16 to 16
- sel_index: int32 [1024], P(('own', 'rep')), may hold values from 0 to 63
- sel_layer: int32 [1024], P(('own', 'rep')), may hold values from 0 to 3, as said below
- counts: int32 [32], P(('own', 'rep')), may hold values from 8 to 32, as said below
Outputs:
- quant_codes: bfloat16 [8, 4, 8, 8, 18432], P('own', 'rep')
- quant_steps: float32 [8, 288], P('own')
- clip_error: float32 [8, 288], P('own')
Inputs may be any that keep to these rules, and one draw needn't show every extreme that they name: `sel_layer`: among the 32 entries of one device, at most 8 name any one layer; the first 8 entries of every device all name one and the same layer. `counts`: some device has all 32 entries live.
All inputs are finite; a program needn't handle non-finite values.
Results may differ from a plain program's by a relative error of at most 0.001.
Values may be sent and summed in bfloat16 or wider, within the bound.
A program may use at most 128 MiB of HBM per device.

v0:
```python
import jax
import jax.numpy as jnp
from jax import lax
from jax.sharding import PartitionSpec as P

SLICES = 2


headroom = 0.5


def slot_table(index_row, layer_row, live_count, group_layer, capacity):
    n_select = index_row.shape[0]
    is_live = jnp.arange(n_select) < live_count
    matches = (layer_row[None, :] == group_layer[:, None]) & is_live[None, :]
    ranking = jnp.cumsum(matches.astype(jnp.int32), axis=1) - 1
    slot_hit = matches[:, None, :] & (ranking[:, None, :] == jnp.arange(capacity)[None, :, None])
    chosen = jnp.sum(jnp.where(slot_hit, index_row[None, None, :], 0), axis=2)
    filled = jnp.any(slot_hit, axis=2)
    return (chosen, filled)


def body(block_pool, sel_index, sel_layer, counts):
    own_count = lax.axis_size("own")
    rep_count = lax.axis_size("rep")
    n_select = sel_index.shape[0]
    capacity = n_select // 4
    block_tokens = block_pool.shape[1]
    latent_width = block_pool.shape[2]
    half_width = latent_width // SLICES
    flat_width = block_tokens * half_width
    layer_count = own_count // SLICES
    layer_ids = jnp.arange(layer_count)
    chosen, filled = slot_table(sel_index, sel_layer, counts[0], layer_ids, capacity)
    pool_rows = block_pool.reshape(block_pool.shape[0], block_tokens * latent_width)
    picked = jnp.take(pool_rows, chosen.reshape(-1), axis=0)
    picked = jnp.where(filled.reshape(-1)[:, None], picked, jnp.zeros((), picked.dtype))
    picked = picked.reshape(layer_count, capacity, block_tokens, SLICES, half_width)
    parted = picked.transpose(0, 3, 1, 2, 4).reshape(own_count, capacity, flat_width)
    denominator = float(own_count * rep_count * capacity * block_tokens)
    arrived = lax.all_to_all(parted, "own", split_axis=0, concat_axis=0, tiled=True)
    flat_peak = jnp.max(jnp.abs(arrived), axis=(0, 1)).astype(jnp.float32)
    local_peak = jnp.max(flat_peak.reshape(block_tokens, half_width), axis=0)
    peak_abs = lax.pmax(local_peak, "rep")
    step_size = headroom * jnp.maximum(peak_abs, 1.0) / 127.0
    step_flat = jnp.tile(step_size, block_tokens)
    values = arrived.astype(jnp.float32)
    encoded = jnp.clip(values / step_flat, -127.0, 127.0).astype(jnp.bfloat16)
    encoded = lax.optimization_barrier(encoded)
    decoded = encoded.astype(jnp.float32) * step_flat
    flat_error = jnp.sum((values - decoded) ** 2, axis=(0, 1))
    sq_error = jnp.sum(flat_error.reshape(block_tokens, half_width), axis=0)
    error_all = lax.psum(sq_error, "rep")
    steps_out = step_size[None, :]
    error_out = (error_all / (step_size * step_size * denominator))[None, :]
    return (encoded[None, None], steps_out, error_out)


def solution(mesh):
    return jax.shard_map(
        body,
        mesh=mesh,
        in_specs=(
            P(("own", "rep"), None, None),
            P(("own", "rep")),
            P(("own", "rep")),
            P(("own", "rep")),
        ),
        out_specs=(P("own", "rep", None, None, None), P("own", None), P("own", None)),
        check_vma=False,
    )
```

profile of v0, /device:TPU:0, one launch (start us, length us, event | category | flops | bytes accessed | tf_op | source)
XLA Modules:
  0.0 115.5 jit_solution(2599126391710674520)
XLA Ops:
  1.3 0.7 fusion.9
  2.0 0.2 reduce_window_sum.11
  2.2 0.1 fusion.6
  2.3 0.8 select_reduce_fusion
  3.1 0.1 reshape.133
  3.2 9.9 %reshape.132 = bf16[64,36864]{1,0:T(8,128)(2,1)} reshape(bf16[64,64,576]{2,1,0:T(8,128)(2,1)} %param.4) | data formatting | bytes 9437184 | tf_op jit(solution)/shard_map/reshape | solution.py:35
  13.2 8.4 %gather_fusion = bf16[32,36864]{1,0:T(8,128)(2,1)} fusion(bf16[64,36864]{1,0:T(8,128)(2,1)} %reshape.132, s32[1024]{0:T(1024)S(1)} %pad_clamp_fusion), kind=kCustom, calls=%fused_computation | custom fusion | bytes 4718720 | tf_op jit(solution)/shard_map/jit(_take)/gather | solution.py:36
  21.5 6.7 %gather.7 = bf16[4,8,64,2,288]{4,3,2,1,0:T(2,128)(2,1)S(1)} reshape(bf16[32,36864]{1,0:T(8,128)(2,1)} %gather_fusion) | data formatting | bytes 4718592 | tf_op jit(solution)/shard_map/jit(_take)/gather | solution.py:36
  28.3 3.1 %fusion.4 = bf16[4,2,8,64,288]{4,1,3,2,0:T(2,128)(2,1)S(1)} fusion(pred[4,8]{1,0:T(4,128)(4,1)S(1)} %fusion.6, bf16[4,8,64,2,288]{4,3,2,1,0:T(2,128)(2,1)S(1)} %gather.7, pred[4,8]{1,0:T(4,128)(4,1)S(1)} %compare_and_fusion), kind=kLoop, calls=%fused_computation.9 | loop fusion | flops 2359296 | bytes 4718656 | tf_op jit(solution)/shard_map/transpose | solution.py:39
  31.4 0.7 copy.8
  32.1 5.0 %reshape.134 = bf16[8,8,18432]{2,1,0:T(8,128)(2,1)} reshape(bf16[4,2,8,64,288]{4,3,2,1,0:T(8,128)(2,1)S(1)} %copy.8) | data formatting | bytes 4718592 | tf_op jit(solution)/shard_map/reshape | solution.py:39
  37.1 61.1 %all_to_all.5 = bf16[8,8,18432]{2,1,0:T(8,128)(2,1)S(1)} all-to-all(bf16[8,8,18432]{2,1,0:T(8,128)(2,1)} %reshape.134), channel_id=1, replica_groups=mesh['own'=8,'rep'=4] {'own'}, dimensions={0} | all-to-all | bytes 4718592 | tf_op jit(solution)/shard_map/all_to_all | solution.py:41
  98.2 0.4 abs_reduce_fusion
  98.6 0.1 reduce_max.26
  98.8 5.7 %pmax.7 = f32[288]{0:T(512)S(1)} all-reduce(bf16[288]{0:T(512)(128)(2,1)S(1)} %reduce_max.27), channel_id=1, replica_groups=mesh['own'=8,'rep'=4] {'rep'}, use_global_device_ids=true, to_apply=%region_5.6 | all-reduce | flops 288 | bytes 1728 | tf_op jit(solution)/shard_map/pmax | solution.py:44
  104.4 0.6 tile.9
  105.0 0.1 div.21
  105.1 0.6 fusion.1
  105.7 0.0 copy-start
  105.7 1.4 %copy-done = bf16[8,8,18432]{2,1,0:T(8,128)(2,1)} copy-done((bf16[8,8,18432]{2,1,0:T(8,128)(2,1)}, bf16[8,8,18432]{2,1,0:T(8,128)(2,1)S(1)}, u32[]{:S(2)}) %copy-start) | copy-done | bytes 2359320
  107.1 1.0 fusion.3
  108.1 0.1 reshape.135
  108.3 6.7 %psum.7 = f32[288]{0:T(512)S(1)} all-reduce(f32[288]{0:T(512)S(1)} %reduce_sum.29), channel_id=1, replica_groups=mesh['own'=8,'rep'=4] {'rep'}, use_global_device_ids=true, to_apply=%region_8.9 | all-reduce | flops 288 | bytes 2304 | tf_op jit(solution)/shard_map/psum | solution.py:53
  114.9 0.6 broadcast_in_dim.55
  (10 shorter events, 0.1 us)
Async XLA Ops:
  105.7 1.4 %copy-start = (bf16[8,8,18432]{2,1,0:T(8,128)(2,1)}, bf16[8,8,18432]{2,1,0:T(8,128)(2,1)S(1)}, u32[]{:S(2)}) copy-start(bf16[8,8,18432]{2,1,0:T(8,128)(2,1)S(1)} %fusion.1) | copy-start | bytes 7077892
where the time goes:
time: 116 us
  blocking collectives  73.4 us (63%)
  local copies, waits for them, and re-layouts  33.7 us (29%)
  other arithmetic  7.03 us (6%)
  between operations  1.35 us (1%)
    all_to_all x1, blocking collectives, body(): lax.all_to_all(parted, 'own', split_axis=0, concat_axis=0, tiled=True)  61.1 us
    gather x2, local copies, waits for them, and re-layouts, body(): picked = jnp.take(pool_rows, chosen.reshape(-1), axis=0)  15.1 us
    reshape x1, local copies, waits for them, and re-layouts, body(): block_pool.reshape(block_pool.shape[0], block_tokens * latent_width)  9.91 us
    psum x1, blocking collectives, body(): error_all = lax.psum(sq_error, 'rep')  6.65 us
    pmax x1, blocking collectives, body(): peak_abs = lax.pmax(local_peak, 'rep')  5.66 us
    reshape x1, local copies, waits for them, and re-layouts, body(): picked.transpose(0, 3, 1, 2, 4).reshape(own_count, capacity, flat_width)  4.99 us
    transpose x1, other arithmetic, body(): picked.transpose(0, 3, 1, 2, 4).reshape(own_count, capacity, flat_width)  3.1 us

commit v1 on v0

v1 whole, which is shorter than its diff:
```python
import functools
import math

import jax
import jax.numpy as jnp
from jax import lax
from jax.experimental import pallas as pl
from jax.experimental.pallas import tpu as pltpu
from jax.sharding import PartitionSpec as P

SLICES = 2
LANES = 128
headroom = 0.5


def slot_table(index_row, layer_row, live_count, group_layer, capacity, empty):
    n_select = index_row.shape[0]
    is_live = jnp.arange(n_select) < live_count
    matches = (layer_row[None, :] == group_layer[:, None]) & is_live[None, :]
    earlier = jnp.arange(n_select)[:, None] < jnp.arange(n_select)[None, :]
    ranking = jnp.sum((matches[:, :, None] & earlier[None]).astype(jnp.int32), axis=1)
    slot_hit = matches[:, None, :] & (ranking[:, None, :] == jnp.arange(capacity)[None, :, None])
    chosen = jnp.sum(jnp.where(slot_hit, index_row[None, None, :] - empty, 0), axis=2)
    return chosen + empty


def layer_order(layers):
    half = layers // 2
    return sorted(range(layers), key=lambda k: (k == 0, abs(k - half)))


def kernel(own_n, rep_n, cap, slot_ref, pool_ref, codes_ref, steps_ref, err_ref,
           pool_v, stage, send, recv, coded, pk_send, pk_recv, pk_mine, pk_rep, er_mine, er_rep,
           pool_sem, ssem, rsem, pssem, prsem, rpssem, rprsem, ressem, rersem, out_sem):
    rows, tokens, width = pool_ref.shape
    half = width // SLICES
    flat = tokens * half
    group = LANES // math.gcd(half, LANES)
    period = group * half
    layers = own_n // SLICES
    me = lax.axis_index("own")
    rep = lax.axis_index("rep")
    my_layer = me // SLICES
    my_slice = me % SLICES
    tiles = stage.shape[0]
    denominator = float(own_n * rep_n * cap * tokens)
    pieces = pool_sem.shape[0]
    per_piece = rows // pieces

    loads = [
        pltpu.make_async_copy(
            pool_ref.at[pl.ds(p * per_piece, per_piece)],
            pool_v.at[pl.ds(p * per_piece, per_piece)],
            pool_sem.at[p],
        )
        for p in range(pieces)
    ]
    for load in loads:
        load.start()

    barrier = pltpu.get_barrier_semaphore()
    for k in range(1, own_n):
        pl.semaphore_signal(barrier, inc=1, device_id={"own": lax.rem(me + k, own_n)},
                            device_id_type=pl.DeviceIdType.MESH)
    for k in range(1, rep_n):
        pl.semaphore_signal(barrier, inc=1, device_id={"rep": lax.rem(rep + k, rep_n)},
                            device_id_type=pl.DeviceIdType.MESH)

    pool_v[rows] = jnp.zeros((tokens, width), pool_v.dtype)
    for load in loads:
        load.wait()

    def layer_peak(layer, carry):
        best = jnp.zeros((tokens, width), pool_v.dtype)
        for c in range(cap):
            best = jnp.maximum(best, jnp.abs(pool_v[slot_ref[layer * cap + c]]))
        top = jnp.max(best.astype(jnp.float32), axis=0, keepdims=True)
        for part in range(SLICES):
            one = top[:, part * half:(part + 1) * half]
            pk_send[layer * SLICES + part] = jnp.concatenate([one] * group, axis=1)
        return carry

    lax.fori_loop(0, layers, layer_peak, 0)
    pl.semaphore_wait(barrier, own_n - 1 + rep_n - 1)

    def peak_copy(peer, landing):
        return pltpu.make_async_remote_copy(
            src_ref=pk_send.at[peer], dst_ref=pk_recv.at[landing],
            send_sem=pssem.at[peer], recv_sem=prsem.at[landing],
            device_id={"own": peer}, device_id_type=pl.DeviceIdType.MESH)

    def block_copy(peer, landing):
        return pltpu.make_async_remote_copy(
            src_ref=send.at[peer], dst_ref=recv.at[landing],
            send_sem=ssem.at[peer], recv_sem=rsem.at[landing],
            device_id={"own": peer}, device_id_type=pl.DeviceIdType.MESH)

    for k in range(1, own_n):
        peer = lax.rem(me + k, own_n)
        peak_copy(peer, me).start()

    for off in layer_order(layers):
        layer = lax.rem(my_layer + off, layers)
        for c in range(cap):
            block = pool_v[slot_ref[layer * cap + c]].astype(jnp.float32)
            for q in range(tiles):
                lo, hi = q * LANES, min(width, (q + 1) * LANES)
                stage[q, c * tokens:(c + 1) * tokens, 0:hi - lo] = block[:, lo:hi]

        def flatten(i, carry):
            rows_of = [
                jnp.concatenate(
                    [stage[q, pl.ds(i * group + j, cap, stride=tokens), :] for q in range(tiles)], axis=1)
                for j in range(group)
            ]
            for part in range(SLICES):
                joined = jnp.concatenate([r[:, part * half:(part + 1) * half] for r in rows_of], axis=1)
                at = pl.multiple_of(i * period, period)
                send[layer * SLICES + part, :, pl.ds(at, period)] = joined.astype(send.dtype)
            return carry

        lax.fori_loop(0, tokens // group, flatten, 0)
        if off:
            for part in range(SLICES):
                block_copy(layer * SLICES + part, me).start()
        else:
            for k in range(1, SLICES):
                block_copy(layer * SLICES + lax.rem(my_slice + k, SLICES), me).start()

    best = pk_send[me]
    for k in range(1, own_n):
        src = lax.rem(me + k, own_n)
        peak_copy(src, src).wait_recv()
        best = jnp.maximum(best, pk_recv[src])
    pk_mine[...] = best

    def rep_copy(mine, table, s_sem, r_sem, peer, landing):
        return pltpu.make_async_remote_copy(
            src_ref=mine, dst_ref=table.at[landing],
            send_sem=s_sem.at[peer], recv_sem=r_sem.at[landing],
            device_id={"rep": peer}, device_id_type=pl.DeviceIdType.MESH)

    for k in range(1, rep_n):
        rep_copy(pk_mine, pk_rep, rpssem, rprsem, lax.rem(rep + k, rep_n), rep).start()
    for k in range(1, rep_n):
        src = lax.rem(rep + k, rep_n)
        rep_copy(pk_mine, pk_rep, rpssem, rprsem, src, src).wait_recv()
        best = jnp.maximum(best, pk_rep[src])

    step = headroom * jnp.maximum(best, 1.0) / 127.0
    inverse = 1.0 / step
    steps_ref[...] = step[:, :half]
    step_wide = jnp.broadcast_to(step, (cap, period))
    inv_wide = jnp.broadcast_to(inverse, (cap, period))

    def out_copy(src):
        return pltpu.make_async_copy(coded.at[src], codes_ref.at[0, 0, src], out_sem.at[src])

    def encode(source, src, total):
        def one(i, total):
            at = pl.multiple_of(i * period, period)
            x = source[src, :, pl.ds(at, period)].astype(jnp.float32)
            y = jnp.clip(x * inv_wide, -127.0, 127.0).astype(coded.dtype)
            coded[src, :, pl.ds(at, period)] = y
            diff = x - y.astype(jnp.float32) * step_wide
            return total + diff * diff
        total = lax.fori_loop(0, tokens // group, one, total)
        out_copy(src).start()
        return total

    total = encode(send, me, jnp.zeros((cap, period), jnp.float32))
    for part in range(1, SLICES):
        src = my_layer * SLICES + lax.rem(my_slice + part, SLICES)
        block_copy(src, src).wait_recv()
        total = encode(recv, src, total)
    for off in layer_order(layers)[::-1][1:]:
        layer = lax.rem(my_layer - off + layers, layers)
        for part in range(SLICES):
            src = layer * SLICES + part
            block_copy(src, src).wait_recv()
            total = encode(recv, src, total)

    mine = jnp.sum(total, axis=0, keepdims=True)
    er_mine[...] = mine
    for k in range(1, rep_n):
        rep_copy(er_mine, er_rep, ressem, rersem, lax.rem(rep + k, rep_n), rep).start()
    er_rep[rep] = mine
    for k in range(1, rep_n):
        src = lax.rem(rep + k, rep_n)
        rep_copy(er_mine, er_rep, ressem, rersem, src, src).wait_recv()
    whole = er_rep[0]
    for k in range(1, rep_n):
        whole = whole + er_rep[k]
    folded = whole[:, :half]
    for j in range(1, group):
        folded = folded + whole[:, j * half:(j + 1) * half]
    narrow = step[:, :half]
    err_ref[...] = folded / (narrow * narrow * denominator)

    for k in range(1, own_n):
        peer = lax.rem(me + k, own_n)
        peak_copy(peer, me).wait_send()
        block_copy(peer, me).wait_send()
    for k in range(1, rep_n):
        peer = lax.rem(rep + k, rep_n)
        rep_copy(pk_mine, pk_rep, rpssem, rprsem, peer, rep).wait_send()
        rep_copy(er_mine, er_rep, ressem, rersem, peer, rep).wait_send()
    for src in range(own_n):
        out_copy(src).wait()


def body(block_pool, sel_index, sel_layer, counts):
    own_n = lax.axis_size("own")
    rep_n = lax.axis_size("rep")
    cap = sel_index.shape[0] // 4
    rows, tokens, width = block_pool.shape
    half = width // SLICES
    flat = tokens * half
    group = LANES // math.gcd(half, LANES)
    period = group * half
    layers = own_n // SLICES
    slots = slot_table(sel_index, sel_layer, counts[0], jnp.arange(layers), cap, rows).reshape(-1)
    f32 = jnp.float32
    dma = pltpu.SemaphoreType.DMA
    dtype = block_pool.dtype
    codes, steps, err = pl.pallas_call(
        functools.partial(kernel, own_n, rep_n, cap),
        out_shape=(
            jax.ShapeDtypeStruct((1, 1, own_n, cap, flat), dtype),
            jax.ShapeDtypeStruct((1, half), f32),
            jax.ShapeDtypeStruct((1, half), f32),
        ),
        in_specs=[pl.BlockSpec(memory_space=pltpu.SMEM), pl.BlockSpec(memory_space=pl.ANY)],
        out_specs=(
            pl.BlockSpec(memory_space=pl.ANY),
            pl.BlockSpec(memory_space=pltpu.VMEM),
            pl.BlockSpec(memory_space=pltpu.VMEM),
        ),
        scratch_shapes=[
            pltpu.VMEM((rows + 1, tokens, width), dtype),
            pltpu.VMEM((pl.cdiv(width, LANES), cap * tokens, LANES), f32),
            pltpu.VMEM((own_n, cap, flat), dtype),
            pltpu.VMEM((own_n, cap, flat), dtype),
            pltpu.VMEM((own_n, cap, flat), dtype),
            pltpu.VMEM((own_n, 1, period), f32),
            pltpu.VMEM((own_n, 1, period), f32),
            pltpu.VMEM((1, period), f32),
            pltpu.VMEM((rep_n, 1, period), f32),
            pltpu.VMEM((1, period), f32),
            pltpu.VMEM((rep_n, 1, period), f32),
            dma((8,)),
            dma((own_n,)), dma((own_n,)), dma((own_n,)), dma((own_n,)),
            dma((rep_n,)), dma((rep_n,)), dma((rep_n,)), dma((rep_n,)),
            dma((own_n,)),
        ],
        compiler_params=pltpu.CompilerParams(
            collective_id=0, has_side_effects=True, vmem_limit_bytes=60 * 1024 * 1024),
        name="latent_code",
    )(slots, block_pool)
    return codes, steps, err


def solution(mesh):
    return jax.shard_map(
        body,
        mesh=mesh,
        in_specs=(
            P(("own", "rep"), None, None),
            P(("own", "rep")),
            P(("own", "rep")),
            P(("own", "rep")),
        ),
        out_specs=(P("own", "rep", None, None, None), P("own", None), P("own", None)),
        check_vma=False,
    )
```

time: 116 us -> 73.7 us (0.64)
  the two profiles are of different devices: /device:TPU:0 before, /device:TPU:11 now
where the time goes in v1:
time: 73.7 us; the launch traced here: 73.5 us
  Pallas kernels  65.7 us (89%)
  local copies, waits for them, and re-layouts  4.96 us (7%)
  other arithmetic  1.59 us (2%)
  between operations  1.32 us (2%)
    pallas_call x1, Pallas kernels, body(): pl.pallas_call(functools.partial(kernel, own_n, rep_n, cap), out_shape=(j...  65.7 us
    unnamed x7, local copies, waits for them, and re-layouts  4.36 us

profile of v1, /device:TPU:11, one launch (start us, length us, event | category | flops | bytes accessed | tf_op | source)
XLA Modules:
  0.0 73.5 jit_solution(10193551806548365784)
XLA Ops:
  1.3 0.7 fusion.1
  2.0 0.7 broadcast_add_fusion.1
  2.6 0.1 convert_reduce_fusion
  2.7 0.2 select_reduce_fusion
  2.9 0.6 add.14.slot_ref
  3.5 65.7 %latent_code.1 = (bf16[1,1,8,8,18432]{4,3,2,1,0:T(8,128)(2,1)}, f32[1,288]{1,0:T(1,128)}, f32[1,288]{1,0:T(1,128)}) custom-call(s32[32]{0:T(128)} %add.14.slot_ref, bf16[64,64,576]{2,1,0:T(8,128)(2,1)} %pool_ref.1), custom_call_target="tpu_custom_call" | custom-call | tf_op jit(solution)/shard_map/latent_code/pallas_call | solution.py:226
  69.2 0.0 copy-start.1
  69.2 0.0 copy-start
  69.2 3.2 %copy.11 = bf16[1,1,8,8,18432]{4,3,2,1,0:T(8,128)(2,1)} copy(bf16[1,1,8,8,18432]{4,3,2,1,0:T(8,128)(2,1)} %get-tuple-element.6) | data formatting | bytes 4718592
  72.4 0.0 copy-done.1
  72.4 0.6 copy.12
  73.0 0.0 copy-done
  73.0 0.6 copy.13
  (3 shorter events, 0.0 us)
Async XLA Ops:
  69.2 3.2 %copy-start.1 = (f32[1,288]{1,0:T(1,128)S(1)}, f32[1,288]{1,0:T(1,128)}, u32[]{:S(2)}) copy-start(f32[1,288]{1,0:T(1,128)} %get-tuple-element.7) | copy-start | bytes 3460
  69.2 3.8 %copy-start = (f32[1,288]{1,0:T(1,128)S(1)}, f32[1,288]{1,0:T(1,128)}, u32[]{:S(2)}) copy-start(f32[1,288]{1,0:T(1,128)} %get-tuple-element.8) | copy-start | bytes 3460

commit v2 on v1

--- a/solution.py
+++ b/solution.py
@@ -24,14 +24,16 @@
     return chosen + empty
 
 
-def layer_order(layers):
-    half = layers // 2
-    return sorted(range(layers), key=lambda k: (k == 0, abs(k - half)))
+def partner_layer(my_layer, layers, k):
+    near = layers // 2
+    if k < near:
+        return lax.rem(my_layer + k, near) + (1 - my_layer // near) * near
+    return lax.rem(my_layer + 1 + k - near, near) + (my_layer // near) * near
 
 
 def kernel(own_n, rep_n, cap, slot_ref, pool_ref, codes_ref, steps_ref, err_ref,
-           pool_v, stage, send, recv, coded, pk_send, pk_recv, pk_mine, pk_rep, er_mine, er_rep,
-           pool_sem, ssem, rsem, pssem, prsem, rpssem, rprsem, ressem, rersem, out_sem):
+           pool_v, stage, send, recv, pk_send, pk_recv, pk_mine, pk_rep, er_mine, er_rep,
+           pool_sem, ssem, rsem, pssem, prsem, rpssem, rprsem, ressem, rersem):
     rows, tokens, width = pool_ref.shape
     half = width // SLICES
     flat = tokens * half
@@ -99,8 +101,8 @@
         peer = lax.rem(me + k, own_n)
         peak_copy(peer, me).start()
 
-    for off in layer_order(layers):
-        layer = lax.rem(my_layer + off, layers)
+    for k in range(layers):
+        layer = partner_layer(my_layer, layers, k)
         for c in range(cap):
             block = pool_v[slot_ref[layer * cap + c]].astype(jnp.float32)
             for q in range(tiles):
@@ -120,12 +122,8 @@
             return carry
 
         lax.fori_loop(0, tokens // group, flatten, 0)
-        if off:
-            for part in range(SLICES):
-                block_copy(layer * SLICES + part, me).start()
-        else:
-            for k in range(1, SLICES):
-                block_copy(layer * SLICES + lax.rem(my_slice + k, SLICES), me).start()
+        for part in range(1 if k == layers - 1 else 0, SLICES):
+            block_copy(layer * SLICES + lax.rem(my_slice + part, SLICES), me).start()
 
     best = pk_send[me]
     for k in range(1, own_n):
@@ -153,30 +151,25 @@
     step_wide = jnp.broadcast_to(step, (cap, period))
     inv_wide = jnp.broadcast_to(inverse, (cap, period))
 
-    def out_copy(src):
-        return pltpu.make_async_copy(coded.at[src], codes_ref.at[0, 0, src], out_sem.at[src])
-
     def encode(source, src, total):
         def one(i, total):
             at = pl.multiple_of(i * period, period)
             x = source[src, :, pl.ds(at, period)].astype(jnp.float32)
-            y = jnp.clip(x * inv_wide, -127.0, 127.0).astype(coded.dtype)
-            coded[src, :, pl.ds(at, period)] = y
+            y = jnp.clip(x * inv_wide, -127.0, 127.0).astype(codes_ref.dtype)
+            codes_ref[0, 0, src, :, pl.ds(at, period)] = y
             diff = x - y.astype(jnp.float32) * step_wide
             return total + diff * diff
-        total = lax.fori_loop(0, tokens // group, one, total)
-        out_copy(src).start()
-        return total
+        return lax.fori_loop(0, tokens // group, one, total)
 
     total = encode(send, me, jnp.zeros((cap, period), jnp.float32))
     for part in range(1, SLICES):
         src = my_layer * SLICES + lax.rem(my_slice + part, SLICES)
         block_copy(src, src).wait_recv()
         total = encode(recv, src, total)
-    for off in layer_order(layers)[::-1][1:]:
-        layer = lax.rem(my_layer - off + layers, layers)
+    for k in list(range(layers // 2, layers - 1)) + list(range(layers // 2)):
+        layer = partner_layer(my_layer, layers, k)
         for part in range(SLICES):
-            src = layer * SLICES + part
+            src = layer * SLICES + lax.rem(my_slice + part, SLICES)
             block_copy(src, src).wait_recv()
             total = encode(recv, src, total)
 
@@ -205,8 +198,6 @@
         peer = lax.rem(rep + k, rep_n)
         rep_copy(pk_mine, pk_rep, rpssem, rprsem, peer, rep).wait_send()
         rep_copy(er_mine, er_rep, ressem, rersem, peer, rep).wait_send()
-    for src in range(own_n):
-        out_copy(src).wait()
 
 
 def body(block_pool, sel_index, sel_layer, counts):
@@ -226,20 +217,19 @@
     codes, steps, err = pl.pallas_call(
         functools.partial(kernel, own_n, rep_n, cap),
         out_shape=(
-            jax.ShapeDtypeStruct((1, 1, own_n, cap, flat), dtype),
+            pltpu.VMEM((1, 1, own_n, cap, flat), dtype),
             jax.ShapeDtypeStruct((1, half), f32),
             jax.ShapeDtypeStruct((1, half), f32),
         ),
-        in_specs=[pl.BlockSpec(memory_space=pltpu.SMEM), pl.BlockSpec(memory_space=pl.ANY)],
+        in_specs=[pl.BlockSpec(memory_space=pltpu.SMEM), pl.BlockSpec(memory_space=pltpu.HBM)],
         out_specs=(
-            pl.BlockSpec(memory_space=pl.ANY),
+            pl.BlockSpec(memory_space=pltpu.VMEM),
             pl.BlockSpec(memory_space=pltpu.VMEM),
             pl.BlockSpec(memory_space=pltpu.VMEM),
         ),
         scratch_shapes=[
             pltpu.VMEM((rows + 1, tokens, width), dtype),
             pltpu.VMEM((pl.cdiv(width, LANES), cap * tokens, LANES), f32),
-            pltpu.VMEM((own_n, cap, flat), dtype),
             pltpu.VMEM((own_n, cap, flat), dtype),
             pltpu.VMEM((own_n, cap, flat), dtype),
             pltpu.VMEM((own_n, 1, period), f32),
@@ -251,10 +241,9 @@
             dma((8,)),
             dma((own_n,)), dma((own_n,)), dma((own_n,)), dma((own_n,)),
             dma((rep_n,)), dma((rep_n,)), dma((rep_n,)), dma((rep_n,)),
-            dma((own_n,)),
         ],
         compiler_params=pltpu.CompilerParams(
-            collective_id=0, has_side_effects=True, vmem_limit_bytes=60 * 1024 * 1024),
+            collective_id=0, has_side_effects=True, vmem_limit_bytes=36 * 1024 * 1024),
         name="latent_code",
     )(slots, block_pool)
     return codes, steps, err

time: 73.7 us -> 71.9 us (0.976)
  Pallas kernels: 65.7 us -> 63.6 us
    pallas_call x1, Pallas kernels: 65.7 us -> 63.6 us  [body(): pl.pallas_call(functools.partial(kernel, own_n, rep_n, cap), out_shape=(p...]
    unnamed x7 -> x5, local copies, waits for them, and re-layouts: 4.36 us -> 5.03 us
where the time goes in v2:
time: 71.9 us; the launch traced here: 71.6 us
  Pallas kernels  63.6 us (88%)
  local copies, waits for them, and re-layouts  5.11 us (7%)
  other arithmetic  1.59 us (2%)
  between operations  1.3 us (2%)
    pallas_call x1, Pallas kernels, body(): pl.pallas_call(functools.partial(kernel, own_n, rep_n, cap), out_shape=(p...  63.6 us
    unnamed x5, local copies, waits for them, and re-layouts  5.03 us

profile of v2, /device:TPU:11, one launch (start us, length us, event | category | flops | bytes accessed | tf_op | source)
XLA Modules:
  0.0 71.6 jit_solution(3372811690961660732)
XLA Ops:
  1.3 0.7 fusion.1
  2.0 0.7 broadcast_add_fusion.1
  2.6 0.1 convert_reduce_fusion
  2.7 0.2 select_reduce_fusion
  2.9 0.1 add.14.slot_ref
  3.0 0.0 copy-start
  3.0 2.5 %copy-done = bf16[64,64,576]{2,1,0:T(8,128)(2,1)S(1)} copy-done((bf16[64,64,576]{2,1,0:T(8,128)(2,1)S(1)}, bf16[64,64,576]{2,1,0:T(8,128)(2,1)}, u32[]{:S(2)}) %copy-start) | copy-done | bytes 4718616
  5.5 63.6 %latent_code.1 = (bf16[1,1,8,8,18432]{4,3,2,1,0:T(8,128)(2,1)S(1)}, f32[1,288]{1,0:T(1,128)S(1)}, f32[1,288]{1,0:T(1,128)S(1)}) custom-call(s32[32]{0:T(128)S(1)} %add.14.slot_ref, bf16[64,64,576]{2,1,0:T(8,128)(2,1)S(1)} %copy-done), custom_call_target="tpu_custom_call" | custom-call | tf_op jit(solution)/shard_map/latent_code/pallas_call | solution.py:217
  69.0 1.4 %copy.10 = bf16[1,1,8,8,18432]{4,3,2,1,0:T(8,128)(2,1)} copy(bf16[1,1,8,8,18432]{4,3,2,1,0:T(8,128)(2,1)S(1)} %get-tuple-element.3) | data formatting | bytes 4718592
  70.5 0.6 copy.12
  71.0 0.6 copy.13
  (3 shorter events, 0.0 us)
Async XLA Ops:
  3.0 2.5 %copy-start = (bf16[64,64,576]{2,1,0:T(8,128)(2,1)S(1)}, bf16[64,64,576]{2,1,0:T(8,128)(2,1)}, u32[]{:S(2)}) copy-start(bf16[64,64,576]{2,1,0:T(8,128)(2,1)} %pool_ref.1) | copy-start | bytes 14155780

commit v3 on v2

--- a/solution.py
+++ b/solution.py
@@ -13,17 +13,6 @@
 headroom = 0.5
 
 
-def slot_table(index_row, layer_row, live_count, group_layer, capacity, empty):
-    n_select = index_row.shape[0]
-    is_live = jnp.arange(n_select) < live_count
-    matches = (layer_row[None, :] == group_layer[:, None]) & is_live[None, :]
-    earlier = jnp.arange(n_select)[:, None] < jnp.arange(n_select)[None, :]
-    ranking = jnp.sum((matches[:, :, None] & earlier[None]).astype(jnp.int32), axis=1)
-    slot_hit = matches[:, None, :] & (ranking[:, None, :] == jnp.arange(capacity)[None, :, None])
-    chosen = jnp.sum(jnp.where(slot_hit, index_row[None, None, :] - empty, 0), axis=2)
-    return chosen + empty
-
-
 def partner_layer(my_layer, layers, k):
     near = layers // 2
     if k < near:
@@ -31,9 +20,26 @@
     return lax.rem(my_layer + 1 + k - near, near) + (my_layer // near) * near
 
 
-def kernel(own_n, rep_n, cap, slot_ref, pool_ref, codes_ref, steps_ref, err_ref,
-           pool_v, stage, send, recv, pk_send, pk_recv, pk_mine, pk_rep, er_mine, er_rep,
-           pool_sem, ssem, rsem, pssem, prsem, rpssem, rprsem, ressem, rersem):
+def fill_slots(live, index_row, layer_row, table, layers, cap, empty):
+    n_select = index_row.shape[1]
+    is_live = lax.broadcasted_iota(jnp.int32, (1, n_select), 1) < live
+    before = lax.broadcasted_iota(jnp.int32, (n_select, n_select), 0)
+    after = lax.broadcasted_iota(jnp.int32, (n_select, n_select), 1)
+    earlier = jnp.where(before < after, 1.0, 0.0)
+    wanted = lax.broadcasted_iota(jnp.int32, (layers, n_select), 0)
+    matches = jnp.where((layer_row == wanted) & is_live, 1.0, 0.0)
+    ranking = jnp.dot(matches, earlier, preferred_element_type=jnp.float32)
+    slot = lax.broadcasted_iota(jnp.int32, (cap, n_select), 0).astype(jnp.float32)
+    shifted = index_row.astype(jnp.float32) - float(empty)
+    for layer in range(layers):
+        hit = (ranking[layer:layer + 1] == slot) & (matches[layer:layer + 1] > 0.5)
+        found = jnp.sum(jnp.where(hit, shifted, 0.0), axis=1, keepdims=True) + float(empty)
+        table[layer * cap:(layer + 1) * cap, :] = jnp.broadcast_to(found, (cap, LANES)).astype(jnp.int32)
+
+
+def kernel(own_n, rep_n, cap, live_ref, index_ref, layer_ref, pool_ref, codes_ref, steps_ref, err_ref,
+           table, slots, pool_v, stage, send, recv, pk_send, pk_recv, pk_mine, pk_rep, er_mine, er_rep,
+           table_sem, pool_sem, ssem, rsem, pssem, prsem, rpssem, rprsem, ressem, rersem):
     rows, tokens, width = pool_ref.shape
     half = width // SLICES
     flat = tokens * half
@@ -69,22 +75,26 @@
                             device_id_type=pl.DeviceIdType.MESH)
 
     pool_v[rows] = jnp.zeros((tokens, width), pool_v.dtype)
+    fill_slots(live_ref[0], index_ref[...], layer_ref[...], table, layers, cap, rows)
+    to_scalars = pltpu.make_async_copy(table, slots, table_sem)
+    to_scalars.start()
+    to_scalars.wait()
     for load in loads:
         load.wait()
+
+    def row_of(slot):
+        return jnp.minimum(jnp.maximum(slots[slot, 0], 0), rows)
 
     def layer_peak(layer, carry):
         best = jnp.zeros((tokens, width), pool_v.dtype)
         for c in range(cap):
-            best = jnp.maximum(best, jnp.abs(pool_v[slot_ref[layer * cap + c]]))
+            best = jnp.maximum(best, jnp.abs(pool_v[row_of(layer * cap + c)]))
         top = jnp.max(best.astype(jnp.float32), axis=0, keepdims=True)
         for part in range(SLICES):
             one = top[:, part * half:(part + 1) * half]
             pk_send[layer * SLICES + part] = jnp.concatenate([one] * group, axis=1)
         return carry
 
-    lax.fori_loop(0, layers, layer_peak, 0)
-    pl.semaphore_wait(barrier, own_n - 1 + rep_n - 1)
-
     def peak_copy(peer, landing):
         return pltpu.make_async_remote_copy(
             src_ref=pk_send.at[peer], dst_ref=pk_recv.at[landing],
@@ -97,14 +107,9 @@
             send_sem=ssem.at[peer], recv_sem=rsem.at[landing],
             device_id={"own": peer}, device_id_type=pl.DeviceIdType.MESH)
 
-    for k in range(1, own_n):
-        peer = lax.rem(me + k, own_n)
-        peak_copy(peer, me).start()
-
-    for k in range(layers):
-        layer = partner_layer(my_layer, layers, k)
+    def flatten_layer(layer):
         for c in range(cap):
-            block = pool_v[slot_ref[layer * cap + c]].astype(jnp.float32)
+            block = pool_v[row_of(layer * cap + c)].astype(jnp.float32)
             for q in range(tiles):
                 lo, hi = q * LANES, min(width, (q + 1) * LANES)
                 stage[q, c * tokens:(c + 1) * tokens, 0:hi - lo] = block[:, lo:hi]
@@ -122,8 +127,33 @@
             return carry
 
         lax.fori_loop(0, tokens // group, flatten, 0)
-        for part in range(1 if k == layers - 1 else 0, SLICES):
+
+    def start_blocks(layer, parts):
+        for part in parts:
             block_copy(layer * SLICES + lax.rem(my_slice + part, SLICES), me).start()
+
+    straight, across = range(1), range(1, SLICES)
+    first_far = partner_layer(my_layer, layers, 0)
+    flatten_layer(first_far)
+    pl.semaphore_wait(barrier, own_n - 1 + rep_n - 1)
+    start_blocks(first_far, straight)
+
+    lax.fori_loop(0, layers, layer_peak, 0)
+    for k in range(1, own_n):
+        peer = lax.rem(me + k, own_n)
+        peak_copy(peer, me).start()
+
+    flatten_layer(my_layer)
+    start_blocks(my_layer, across)
+    for k in range(layers // 2, layers - 1):
+        layer = partner_layer(my_layer, layers, k)
+        flatten_layer(layer)
+        start_blocks(layer, range(SLICES))
+    start_blocks(first_far, across)
+    for k in range(1, layers // 2):
+        layer = partner_layer(my_layer, layers, k)
+        flatten_layer(layer)
+        start_blocks(layer, range(SLICES))
 
     best = pk_send[me]
     for k in range(1, own_n):
@@ -210,7 +240,6 @@
     group = LANES // math.gcd(half, LANES)
     period = group * half
     layers = own_n // SLICES
-    slots = slot_table(sel_index, sel_layer, counts[0], jnp.arange(layers), cap, rows).reshape(-1)
     f32 = jnp.float32
     dma = pltpu.SemaphoreType.DMA
     dtype = block_pool.dtype
@@ -221,13 +250,17 @@
             jax.ShapeDtypeStruct((1, half), f32),
             jax.ShapeDtypeStruct((1, half), f32),
         ),
-        in_specs=[pl.BlockSpec(memory_space=pltpu.SMEM), pl.BlockSpec(memory_space=pltpu.HBM)],
+        in_specs=[
+            pl.BlockSpec(memory_space=pltpu.SMEM), pl.BlockSpec(memory_space=pltpu.VMEM),
+            pl.BlockSpec(memory_space=pltpu.VMEM), pl.BlockSpec(memory_space=pltpu.HBM)],
         out_specs=(
             pl.BlockSpec(memory_space=pltpu.VMEM),
             pl.BlockSpec(memory_space=pltpu.VMEM),
             pl.BlockSpec(memory_space=pltpu.VMEM),
         ),
         scratch_shapes=[
+            pltpu.VMEM((layers * cap, LANES), jnp.int32),
+            pltpu.SMEM((layers * cap, LANES), jnp.int32),
             pltpu.VMEM((rows + 1, tokens, width), dtype),
             pltpu.VMEM((pl.cdiv(width, LANES), cap * tokens, LANES), f32),
             pltpu.VMEM((own_n, cap, flat), dtype),
@@ -238,14 +271,14 @@
             pltpu.VMEM((rep_n, 1, period), f32),
             pltpu.VMEM((1, period), f32),
             pltpu.VMEM((rep_n, 1, period), f32),
-            dma((8,)),
+            dma, dma((8,)),
             dma((own_n,)), dma((own_n,)), dma((own_n,)), dma((own_n,)),
             dma((rep_n,)), dma((rep_n,)), dma((rep_n,)), dma((rep_n,)),
         ],
         compiler_params=pltpu.CompilerParams(
-            collective_id=0, has_side_effects=True, vmem_limit_bytes=36 * 1024 * 1024),
+            collective_id=0, has_side_effects=True, vmem_limit_bytes=(63 * 1024 * 1024 - own_n * cap * flat * 2)),
         name="latent_code",
-    )(slots, block_pool)
+    )(counts, sel_index[None], sel_layer[None], block_pool)
     return codes, steps, err
 
 

time: 71.9 us -> 68.5 us (0.953); the launches traced: 71.6 us -> 67.4 us
  local copies, waits for them, and re-layouts: 5.11 us -> 2.54 us
  other arithmetic: 1.59 us -> 0 us
    unnamed x5 -> x7, local copies, waits for them, and re-layouts: 5.03 us -> 2.54 us
where the time goes in v3:
time: 68.5 us; the launch traced here: 67.4 us
  Pallas kernels  63.6 us (93%)
  local copies, waits for them, and re-layouts  2.54 us (4%)
  between operations  1.3 us (2%)
    pallas_call x1, Pallas kernels, body(): pl.pallas_call(functools.partial(kernel, own_n, rep_n, cap), out_shape=(p...  63.6 us
    unnamed x7, local copies, waits for them, and re-layouts  2.54 us

profile of v3, /device:TPU:11, one launch (start us, length us, event | category | flops | bytes accessed | tf_op | source)
XLA Modules:
  0.0 67.4 jit_solution(996613215992107750)
XLA Ops:
  1.3 63.6 %latent_code.1 = (bf16[1,1,8,8,18432]{4,3,2,1,0:T(8,128)(2,1)S(1)}, f32[1,288]{1,0:T(1,128)}, f32[1,288]{1,0:T(1,128)}) custom-call(s32[1]{0:T(128)S(6)} %copy.11.live_ref, s32[1,32]{1,0:T(1,128)} %bitcast.2, s32[1,32]{1,0:T(1,128)} %bitcast.3, bf16[64,64,576]{2,1,0:T(8,128)(2,1)} %pool_ref.1), custom_call_target="tpu_custom_call" | custom-call | tf_op jit(solution)/shard_map/latent_code/pallas_call | solution.py:246
  64.9 0.0 copy-start.1
  64.9 0.0 copy-start
  64.9 1.4 %copy.10 = bf16[1,1,8,8,18432]{4,3,2,1,0:T(8,128)(2,1)} copy(bf16[1,1,8,8,18432]{4,3,2,1,0:T(8,128)(2,1)S(1)} %get-tuple-element.3) | data formatting | bytes 4718592
  66.3 0.0 copy-done.1
  66.3 0.6 copy.12
  66.8 0.0 copy-done
  66.8 0.6 copy.13
Async XLA Ops:
  64.9 1.4 %copy-start.1 = (f32[1,288]{1,0:T(1,128)S(1)}, f32[1,288]{1,0:T(1,128)}, u32[]{:S(2)}) copy-start(f32[1,288]{1,0:T(1,128)} %get-tuple-element.10) | copy-start | bytes 3460
  64.9 2.0 %copy-start = (f32[1,288]{1,0:T(1,128)S(1)}, f32[1,288]{1,0:T(1,128)}, u32[]{:S(2)}) copy-start(f32[1,288]{1,0:T(1,128)} %get-tuple-element.11) | copy-start | bytes 3460

commit v4 on v3

--- a/solution.py
+++ b/solution.py
@@ -18,6 +18,14 @@
     if k < near:
         return lax.rem(my_layer + k, near) + (1 - my_layer // near) * near
     return lax.rem(my_layer + 1 + k - near, near) + (my_layer // near) * near
+
+
+def send_order(layers):
+    straight, across, both = range(1), range(1, SLICES), range(SLICES)
+    own = [(layers - 1, across)]
+    near = [(k, both) for k in range(layers // 2, layers - 1)]
+    far = [(k, part) for k in range(1, layers // 2) for part in (across, straight)]
+    return [(0, across), (0, straight)] + near + far + own
 
 
 def fill_slots(live, index_row, layer_row, table, layers, cap, empty):
@@ -132,28 +140,20 @@
         for part in parts:
             block_copy(layer * SLICES + lax.rem(my_slice + part, SLICES), me).start()
 
-    straight, across = range(1), range(1, SLICES)
-    first_far = partner_layer(my_layer, layers, 0)
-    flatten_layer(first_far)
-    pl.semaphore_wait(barrier, own_n - 1 + rep_n - 1)
-    start_blocks(first_far, straight)
-
-    lax.fori_loop(0, layers, layer_peak, 0)
-    for k in range(1, own_n):
-        peer = lax.rem(me + k, own_n)
-        peak_copy(peer, me).start()
-
-    flatten_layer(my_layer)
-    start_blocks(my_layer, across)
-    for k in range(layers // 2, layers - 1):
+    flattened = set()
+    for place, (k, parts) in enumerate(send_order(layers)):
         layer = partner_layer(my_layer, layers, k)
-        flatten_layer(layer)
-        start_blocks(layer, range(SLICES))
-    start_blocks(first_far, across)
-    for k in range(1, layers // 2):
-        layer = partner_layer(my_layer, layers, k)
-        flatten_layer(layer)
-        start_blocks(layer, range(SLICES))
+        if k not in flattened:
+            flatten_layer(layer)
+            flattened.add(k)
+        if not place:
+            pl.semaphore_wait(barrier, own_n - 1 + rep_n - 1)
+        for part in parts:
+            block_copy(layer * SLICES + lax.rem(my_slice + part, SLICES), me).start()
+        if place == 1:
+            lax.fori_loop(0, layers, layer_peak, 0)
+            for step in range(1, own_n):
+                peak_copy(lax.rem(me + step, own_n), me).start()
 
     best = pk_send[me]
     for k in range(1, own_n):
@@ -228,6 +228,18 @@
         peer = lax.rem(rep + k, rep_n)
         rep_copy(pk_mine, pk_rep, rpssem, rprsem, peer, rep).wait_send()
         rep_copy(er_mine, er_rep, ressem, rersem, peer, rep).wait_send()
+
+
+def write_out(codes_v, steps_v, err_v, codes_ref, steps_ref, err_ref, sems):
+    own_n = codes_v.shape[2]
+    moves = [pltpu.make_async_copy(codes_v.at[0, 0, src], codes_ref.at[0, 0, src], sems.at[src])
+             for src in range(own_n)]
+    moves.append(pltpu.make_async_copy(steps_v, steps_ref, sems.at[own_n]))
+    moves.append(pltpu.make_async_copy(err_v, err_ref, sems.at[own_n + 1]))
+    for move in moves:
+        move.start()
+    for move in moves:
+        move.wait()
 
 
 def body(block_pool, sel_index, sel_layer, counts):
@@ -247,8 +259,8 @@
         functools.partial(kernel, own_n, rep_n, cap),
         out_shape=(
             pltpu.VMEM((1, 1, own_n, cap, flat), dtype),
-            jax.ShapeDtypeStruct((1, half), f32),
-            jax.ShapeDtypeStruct((1, half), f32),
+            pltpu.VMEM((1, half), f32),
+            pltpu.VMEM((1, half), f32),
         ),
         in_specs=[
             pl.BlockSpec(memory_space=pltpu.SMEM), pl.BlockSpec(memory_space=pltpu.VMEM),
@@ -279,7 +291,16 @@
             collective_id=0, has_side_effects=True, vmem_limit_bytes=(63 * 1024 * 1024 - own_n * cap * flat * 2)),
         name="latent_code",
     )(counts, sel_index[None], sel_layer[None], block_pool)
-    return codes, steps, err
+    hbm = pl.BlockSpec(memory_space=pltpu.HBM)
+    return pl.pallas_call(
+        write_out,
+        out_shape=tuple(jax.ShapeDtypeStruct(x.shape, x.dtype) for x in (codes, steps, err)),
+        in_specs=[pl.BlockSpec(memory_space=pltpu.VMEM)] * 3,
+        out_specs=(hbm, hbm, hbm),
+        scratch_shapes=[dma((own_n + 2,))],
+        compiler_params=pltpu.CompilerParams(vmem_limit_bytes=4 * 1024 * 1024),
+        name="write_out",
+    )(codes, steps, err)
 
 
 def solution(mesh):

time: 68.5 us -> 66.3 us (0.968); the launches traced: 67.4 us -> 66.1 us
  local copies, waits for them, and re-layouts: 2.54 us -> 0 us
  Pallas kernels: 63.6 us -> 64.9 us
    unnamed x7 -> x0, local copies, waits for them, and re-layouts: 2.54 us -> none
    pallas_call x0 -> x1, Pallas kernels: none -> 1.49 us  [body(): pl.pallas_call(write_out, out_shape=tuple((jax.ShapeDtypeStruct(x.shape,...]
where the time goes in v4:
time: 66.3 us; the launch traced here: 66.1 us
  Pallas kernels  64.9 us (98%)
  between operations  1.29 us (2%)
    pallas_call x1, Pallas kernels, body(): pl.pallas_call(functools.partial(kernel, own_n, rep_n, cap), out_shape=(p...  63.4 us
    pallas_call x1, Pallas kernels, body(): pl.pallas_call(write_out, out_shape=tuple((jax.ShapeDtypeStruct(x.shape,...  1.49 us

profile of v4, /device:TPU:11, one launch (start us, length us, event | category | flops | bytes accessed | tf_op | source)
XLA Modules:
  0.0 66.1 jit_solution(3241313238759892389)
XLA Ops:
  1.3 63.4 %latent_code.1 = (bf16[1,1,8,8,18432]{4,3,2,1,0:T(8,128)(2,1)S(1)}, f32[1,288]{1,0:T(1,128)S(1)}, f32[1,288]{1,0:T(1,128)S(1)}) custom-call(s32[1]{0:T(128)S(6)} %copy.7.live_ref, s32[1,32]{1,0:T(1,128)} %bitcast.2, s32[1,32]{1,0:T(1,128)} %bitcast.3, bf16[64,64,576]{2,1,0:T(8,128)(2,1)} %pool_ref.1), custom_call_target="tpu_custom_call" | custom-call | tf_op jit(solution)/shard_map/latent_code/pallas_call | solution.py:258
  64.7 1.5 %write_out.1 = (bf16[1,1,8,8,18432]{4,3,2,1,0:T(8,128)(2,1)}, f32[1,288]{1,0:T(1,128)}, f32[1,288]{1,0:T(1,128)}) custom-call(bf16[1,1,8,8,18432]{4,3,2,1,0:T(8,128)(2,1)S(1)} %get-tuple-element.6.codes_v, f32[1,288]{1,0:T(1,128)S(1)} %get-tuple-element.7.steps_v, f32[1,288]{1,0:T(1,128)S(1)} %get-tuple-element.8.err_v), custom_call_target="tpu_custom_call" | custom-call | tf_op jit(solution)/shard_map/write_out/pallas_call | solution.py:295
